TPU v7x, 128 devices: a whole 4x4x4 slice. The times are simulated.
128 devices in a mesh: mem: 16 (over y, x), pix: 8 (over z, core).
Axes of the slice: x: 4, y: 4, z: 4, core: 2. Of those that a mesh axis runs over, the one named last changes fastest.
Arguments:
- prior_motion: bfloat16 [64, 16, 262144], P('mem', None, 'pix'), may hold values from -6 to 6
- measured_motion: float32 [1200], replicated, may hold values from -1.6 to 1.6
- measurement_noise_stddev: float32 [1200], replicated, may hold values from 0.05 to 0.5
- gaussian_jitter: float32 [2, 1200, 64], replicated, may hold values from -6 to 6
- scene_couples: int32 [2, 1200], replicated, may hold values from 0 to 15, as said below
- targeted_tile_number: int32 [1200], replicated, may hold values from 0 to 4095
Outputs:
- analysis: bfloat16 [64, 16, 262144], P('mem', None, 'pix')
Inputs may be any that keep to these rules, and one draw needn't show every extreme that they name: scene_couples[0, k] < scene_couples[1, k]: row 0 holds the earlier acquisition, row 1 the later.
All inputs are finite; a program needn't handle non-finite values.
Results may differ from a plain program's by a relative error of at most 0.011.
Values may be sent and summed in bfloat16 or wider, within the bound.
A program may use at most 128 MiB of HBM per device.

v0:
```python
import math
import jax
import jax.numpy as jnp
from jax import lax
from jax.sharding import PartitionSpec as P

BLK = 64
PASS_COUNT = 2


def block_sums(pieces):
    part_cells = pieces.shape[2]
    block_count = part_cells // BLK
    summer = (
        jnp.arange(part_cells, dtype=jnp.int32)[:, None] // BLK
        == jnp.arange(block_count, dtype=jnp.int32)[None, :]
    ).astype(jnp.bfloat16)
    flat = jnp.dot(pieces.reshape(-1, part_cells), summer, preferred_element_type=jnp.float32)
    return flat.reshape(pieces.shape[0], pieces.shape[1], block_count)


def with_sums(pieces):
    return (pieces, block_sums(pieces))


def to_pixels(ground_motion_vector):
    return with_sums(
        lax.all_to_all(ground_motion_vector, "mem", split_axis=2, concat_axis=0, tiled=True)
    )


def to_members(pixel_state):
    return lax.all_to_all(pixel_state, "mem", split_axis=0, concat_axis=2, tiled=True)


def predict(sums, picker):
    flat_sums = sums.reshape(sums.shape[0], -1)
    return (
        jnp.dot(
            picker, flat_sums.T, precision=lax.Precision.HIGHEST, preferred_element_type=jnp.float32
        )
        / BLK
    )


def member_terms(predicted, measured_motion, member_anomaly, noise):
    realization_vectors = predicted.shape[1]
    centred = predicted - jnp.mean(predicted, axis=1, keepdims=True)
    scaled = centred / (member_anomaly[:, None] * math.sqrt(realization_vectors - 1))
    misfit = (
        measured_motion[:, None] + member_anomaly[:, None] * noise - predicted
    ) / member_anomaly[:, None]
    return (scaled, misfit)


def products(scaled, misfit):
    gram = jnp.dot(
        scaled.T, scaled, precision=lax.Precision.HIGHEST, preferred_element_type=jnp.float32
    )
    cross = jnp.dot(
        scaled.T, misfit, precision=lax.Precision.HIGHEST, preferred_element_type=jnp.float32
    )
    return (gram, cross)


def solve_mixing(gram, cross):
    realization_vectors = gram.shape[0]
    factor = jnp.linalg.cholesky(jnp.eye(realization_vectors, dtype=jnp.float32) + gram)
    return (
        jax.scipy.linalg.cho_solve((factor, True), cross) / math.sqrt(realization_vectors - 1)
    ).astype(jnp.bfloat16)


def update(pixel_state, mixing):
    realization_vectors = pixel_state.shape[0]
    average = jnp.sum(pixel_state, axis=0, dtype=jnp.float32) / realization_vectors
    anomaly = (pixel_state.astype(jnp.float32) - average).astype(jnp.bfloat16)
    change = jnp.dot(
        mixing.T, anomaly.reshape(realization_vectors, -1), preferred_element_type=jnp.float32
    )
    return (pixel_state.astype(jnp.float32) + change.reshape(pixel_state.shape)).astype(
        jnp.bfloat16
    )


def body(
    prior_motion,
    measured_motion,
    measurement_noise_stddev,
    gaussian_jitter,
    scene_couples,
    targeted_tile_number,
):
    cells_per_tile = prior_motion.shape[2]
    part_width = cells_per_tile // lax.axis_size("mem")
    local_blocks = part_width // BLK
    first_block = (
        lax.axis_index("pix") * cells_per_tile + lax.axis_index("mem") * part_width
    ) // BLK
    block_range = first_block + jnp.arange(local_blocks, dtype=jnp.int32)
    block_table = (targeted_tile_number[:, None] == block_range[None, :]).astype(jnp.float32)
    scene_timeline = jnp.arange(prior_motion.shape[1], dtype=jnp.int32)
    pair_table = (scene_timeline[None, :] == scene_couples[1][:, None]).astype(jnp.float32) - (
        scene_timeline[None, :] == scene_couples[0][:, None]
    ).astype(jnp.float32)
    picker = (pair_table[:, :, None] * block_table[:, None, :]).reshape(pair_table.shape[0], -1)
    member_anomaly = jnp.sqrt(jnp.float32(float(PASS_COUNT))) * measurement_noise_stddev
    pixel_state, sums = to_pixels(prior_motion)
    for iteration in range(PASS_COUNT):
        if iteration > 0:
            sums = block_sums(pixel_state)
        predicted = predict(sums, picker)
        scaled, misfit = member_terms(
            predicted, measured_motion, member_anomaly, gaussian_jitter[iteration]
        )
        gram, cross = lax.psum(products(scaled, misfit), ("mem", "pix"))
        pixel_state = update(pixel_state, solve_mixing(gram, cross))
    return to_members(pixel_state)


def solution(mesh):
    return jax.shard_map(
        body,
        mesh=mesh,
        in_specs=(P("mem", None, "pix"), P(), P(), P(), P(), P()),
        out_specs=P("mem", None, "pix"),
        check_vma=False,
    )
```

profile of v0, /device:TPU:0, one launch (start us, length us, event | category | flops | bytes accessed | tf_op | source)
XLA Modules:
  0.0 537.7 jit_solution(16468579744521945431)
XLA Ops:
  0.0 37.7 %copy.41 = bf16[4,16,32768]{1,0,2:T(4,128)(2,1)} copy(bf16[4,16,32768]{2,1,0:T(8,128)(2,1)} %param.9) | data formatting | bytes 8388608 | tf_op args[0]
  37.7 36.8 %reshape.195 = bf16[16,2,65536]{2,1,0:T(2,128)(2,1)} reshape(bf16[32768,4,16]{2,1,0:T(4,128)(2,1)} %bitcast.107) | data formatting | bytes 8388608
  74.6 7.3 %all-to-all-start = ((bf16[16,2,65536]{2,1,0:T(2,128)(2,1)}), bf16[16,2,65536]{2,1,0:T(2,128)(2,1)}, u32[]{:S(2)}, u32[]{:S(2)}) async-start(bf16[16,2,65536]{2,1,0:T(2,128)(2,1)} %reshape.195), calls=%async_computation | async-start | bytes 8388608 | tf_op jit(solution)/shard_map/all_to_all | solution.py:28
  82.4 62.8 %all-to-all-done = bf16[16,2,65536]{2,1,0:T(2,128)(2,1)} async-done(((bf16[16,2,65536]{2,1,0:T(2,128)(2,1)}), bf16[16,2,65536]{2,1,0:T(2,128)(2,1)}, u32[]{:S(2)}, u32[]{:S(2)}) %all-to-all-start) | async-done | bytes 4194336 | tf_op jit(solution)/shard_map/all_to_all | solution.py:28
  145.2 25.6 %reshape.196 = bf16[32768,4,16]{2,1,0:T(4,128)(2,1)} reshape(bf16[16,2,65536]{2,1,0:T(2,128)(2,1)} %all-to-all-done) | data formatting | bytes 8388608
  170.8 44.3 %copy.66 = bf16[4,16,16,2048]{3,1,0,2:T(8,128)(2,1)} copy(bf16[4,16,16,2048]{1,0,3,2:T(4,128)(2,1)} %bitcast.105) | data formatting | bytes 8388608 | tf_op jit(solution)/shard_map/all_to_all | solution.py:28
  215.1 33.7 %copy.65 = bf16[4,16,16,2048]{3,2,1,0:T(8,128)(2,1)} copy(bf16[4,16,16,2048]{1,0,3,2:T(4,128)(2,1)} %bitcast.106) | data formatting | bytes 8388608 | tf_op jit(solution)/shard_map/all_to_all | solution.py:28
  248.9 3.4 bitcast_convert_fusion
  255.5 8.1 %copy.48 = f32[16,4,16,2048]{3,2,1,0:T(8,128)} copy(f32[16,4,16,2048]{3,0,2,1:T(8,128)S(1)} %bitcast_convert_fusion) | data formatting | bytes 16777216 | tf_op jit(solution)/shard_map/convert_element_type | solution.py:81
  263.6 12.4 %copy.43 = f32[16,4,16,2048]{3,1,0,2:T(4,128)} copy(f32[16,4,16,2048]{3,0,2,1:T(8,128)} %copy-done) | data formatting | bytes 16777216 | tf_op jit(solution)/shard_map/convert_element_type | solution.py:81
  276.0 3.5 convolution_bitcast_fusion
  282.8 65.0 %all-reduce.1 = (f32[64,64]{1,0:T(8,128)S(1)}, f32[64,64]{0,1:T(8,128)S(1)}) all-reduce(f32[64,64]{1,0:T(8,128)S(1)} %fusion.25, f32[64,64]{0,1:T(8,128)S(1)} %fusion.29), channel_id=1, replica_groups=mesh['mem'=16,'pix'=8] {'mem','pix'}, use_global_device_ids=true, to_apply=%region_4.6 | all-reduce | flops 8192 | bytes 65536 | tf_op jit(solution)/shard_map/psum | solution.py:116
  347.9 5.8 %cholesky.44 = f32[64,64]{1,0:T(8,128)S(1)} custom-call(f32[64,64]{1,0:T(8,128)S(1)} %fusion.52), custom_call_target="Cholesky" | custom-call | tf_op jit(solution)/shard_map/jit(cholesky)/cholesky | solution.py:68
  355.1 4.9 custom-call.8
  360.4 11.6 %copy.73 = f32[8,8,16,2048]{3,1,2,0:T(8,128)} copy(f32[8,8,16,2048]{3,2,1,0:T(8,128)} %bitcast.108) | data formatting | bytes 16777216
  372.1 10.2 %reshape.189 = f32[64,16,2048]{2,0,1:T(8,128)} reshape(f32[16,4,16,2048]{3,1,0,2:T(4,128)} %copy.43) | data formatting | bytes 16777216 | tf_op jit(solution)/shard_map/convert_element_type | solution.py:81
  382.3 4.1 subtract_convert_fusion
  389.5 2.3 copy.51
  396.1 64.4 %all-reduce = (f32[64,64]{1,0:T(8,128)S(1)}, f32[64,64]{0,1:T(8,128)S(1)}) all-reduce(f32[64,64]{1,0:T(8,128)S(1)} %fusion.20, f32[64,64]{0,1:T(8,128)S(1)} %fusion.30), channel_id=1, replica_groups=mesh['mem'=16,'pix'=8] {'mem','pix'}, use_global_device_ids=true, to_apply=%region_8.11 | all-reduce | flops 8192 | bytes 65536 | tf_op jit(solution)/shard_map/psum | solution.py:116
  460.7 5.8 %cholesky.55 = f32[64,64]{1,0:T(8,128)S(1)} custom-call(f32[64,64]{1,0:T(8,128)S(1)} %fusion.48), custom_call_target="Cholesky" | custom-call | tf_op jit(solution)/shard_map/jit(cholesky)/cholesky | solution.py:68
  468.0 4.9 custom-call.9
  473.3 5.0 fusion.1
  480.7 54.4 %all_to_all.33 = bf16[64,16,2048]{2,1,0:T(8,128)(2,1)S(1)} all-to-all(bf16[64,16,2048]{2,1,0:T(8,128)(2,1)S(1)} %copy.58), channel_id=1, replica_groups=mesh['mem'=16,'pix'=8] {'mem'}, dimensions={0} | all-to-all | bytes 8388608 | tf_op jit(solution)/shard_map/all_to_all | solution.py:33
  535.1 2.3 copy.72
  (60 shorter events, 20.3 us)
Async XLA Ops:
  74.6 7.4 %copy-start.4 = (s32[2,1200]{1,0:T(2,128)S(1)}, s32[2,1200]{1,0:T(2,128)}, u32[]{:S(2)}) copy-start(s32[2,1200]{1,0:T(2,128)} %param.13) | copy-start | bytes 28804
  74.6 7.5 %copy-start.6 = (s32[1200]{0:T(1024)S(1)}, s32[1200]{0:T(1024)}, u32[]{:S(2)}) copy-start(s32[1200]{0:T(1024)} %param.14) | copy-start | bytes 14404
  74.6 70.6 %all-to-all-start = ((bf16[16,2,65536]{2,1,0:T(2,128)(2,1)}), bf16[16,2,65536]{2,1,0:T(2,128)(2,1)}, u32[]{:S(2)}, u32[]{:S(2)}) async-start(bf16[16,2,65536]{2,1,0:T(2,128)(2,1)} %reshape.195), calls=%async_computation | async-start | bytes 8388608 | tf_op jit(solution)/shard_map/all_to_all | solution.py:28
  248.9 3.5 copy-start.1
  252.3 3.2 copy-start
  276.0 5.8 %copy-start.5 = (f32[1200]{0:T(1024)S(1)}, f32[1200]{0:T(1024)}, u32[]{:S(2)}) copy-start(f32[1200]{0:T(1024)} %param.11) | copy-start | bytes 14404
  276.0 6.3 %copy-start.9 = (f32[1200]{0:T(1024)S(1)}, f32[1200]{0:T(1024)}, u32[]{:S(2)}) copy-start(f32[1200]{0:T(1024)} %param.10) | copy-start | bytes 14404
  280.0 2.3 copy-start.7
  382.3 5.8 %copy-start.2 = (f32[64,16,2048]{2,0,1:T(8,128)S(1)}, f32[64,16,2048]{2,0,1:T(8,128)}, u32[]{:S(2)}) copy-start(f32[64,16,2048]{2,0,1:T(8,128)} %reshape.189) | copy-start | bytes 25165828
  389.5 2.3 copy-start.3
  393.4 2.2 copy-start.8
where the time goes:
time: 546 us; the launch traced here: 538 us
  local copies, waits for them, and re-layouts  232 us (42%)
  blocking collectives  184 us (34%)
  waiting for transfers between devices  62.8 us (12%)
  other arithmetic  33.1 us (6%)
  matrix products  17.5 us (3%)
  starting transfers between devices  7.33 us (1%)
    psum x2, blocking collectives, body(): gram, cross = lax.psum(products(scaled, misfit), ('mem', 'pix'))  129 us
    unnamed x25, local copies, waits for them, and re-layouts  116 us
    all_to_all x2, local copies, waits for them, and re-layouts, to_pixels(): lax.all_to_all(ground_motion_vector, 'mem', split_axis=2, concat_axis=0,...  78.1 us
    all_to_all x1, waiting for transfers between devices, to_pixels(): lax.all_to_all(ground_motion_vector, 'mem', split_axis=2, concat_axis=0,...  62.8 us
    all_to_all x1, blocking collectives, to_members(): lax.all_to_all(pixel_state, 'mem', split_axis=0, concat_axis=2, tiled=True)  54.4 us
    convert_element_type x3, local copies, waits for them, and re-layouts, update(): pixel_state.astype(jnp.float32) + change.reshape(pixel_state.shape)  30.7 us
    another operation x6, other arithmetic, solve_mixing(): jnp.linalg.cholesky(jnp.eye(realization_vectors, dtype=jnp.float32) + gram)  13.1 us
    another operation x4, other arithmetic, solve_mixing(): jax.scipy.linalg.cho_solve((factor, True), cross)  11.1 us
  transfers between devices with their start and end apart: 1, of which 1 were waited for; matrix products, arithmetic and copies ran while one was open for 0% of the time, Pallas kernels for 0%

commit v1 on v0

--- a/solution.py
+++ b/solution.py
@@ -25,7 +25,15 @@
 
 def to_pixels(ground_motion_vector):
     return with_sums(
-        lax.all_to_all(ground_motion_vector, "mem", split_axis=2, concat_axis=0, tiled=True)
+        jnp.concatenate(
+            lax.all_to_all(
+                jnp.stack(jnp.split(ground_motion_vector, lax.axis_size("mem"), axis=2)),
+                "mem",
+                0,
+                0,
+            ),
+            axis=0,
+        )
     )
 
 

time: 546 us -> 354 us (0.65); the launches traced: 538 us -> 353 us
  local copies, waits for them, and re-layouts: 232 us -> 39.4 us
  matrix products: 17.5 us -> 25.6 us
    unnamed x25 -> x29, local copies, waits for them, and re-layouts: 116 us -> 30.1 us
    all_to_all x2 -> x0, local copies, waits for them, and re-layouts: 78.1 us -> none  [to_pixels(): lax.all_to_all(ground_motion_vector, 'mem', split_axis=2, concat_axis=0,...]
    convert_element_type x3 -> x0, local copies, waits for them, and re-layouts: 30.7 us -> none  [update(): pixel_state.astype(jnp.float32) + change.reshape(pixel_state.shape)]
    dot_general x2, matrix products: 6.43 us -> 13.5 us  [update(): jnp.dot(mixing.T, anomaly.reshape(realization_vectors, -1), preferred_ele...]
where the time goes in v1:
time: 354 us; the launch traced here: 353 us
  blocking collectives  184 us (52%)
  waiting for transfers between devices  62.8 us (18%)
  local copies, waits for them, and re-layouts  39.4 us (11%)
  other arithmetic  33.4 us (9%)
  matrix products  25.6 us (7%)
  starting transfers between devices  7.33 us (2%)
    psum x2, blocking collectives, body(): gram, cross = lax.psum(products(scaled, misfit), ('mem', 'pix'))  129 us
    all_to_all x1, waiting for transfers between devices, to_pixels(): lax.all_to_all(jnp.stack(jnp.split(ground_motion_vector, lax.axis_size('m...  62.8 us
    all_to_all x1, blocking collectives, to_members(): lax.all_to_all(pixel_state, 'mem', split_axis=0, concat_axis=2, tiled=True)  54.6 us
    unnamed x29, local copies, waits for them, and re-layouts  30.1 us
    dot_general x2, matrix products, update(): jnp.dot(mixing.T, anomaly.reshape(realization_vectors, -1), preferred_ele...  13.5 us
    another operation x6, other arithmetic, solve_mixing(): jnp.linalg.cholesky(jnp.eye(realization_vectors, dtype=jnp.float32) + gram)  13.1 us
    another operation x4, other arithmetic, solve_mixing(): jax.scipy.linalg.cho_solve((factor, True), cross)  11.1 us
    all_to_all x1, starting transfers between devices, to_pixels(): lax.all_to_all(jnp.stack(jnp.split(ground_motion_vector, lax.axis_size('m...  7.33 us
  transfers between devices with their start and end apart: 1, of which 1 were waited for; matrix products, arithmetic and copies ran while one was open for 0% of the time, Pallas kernels for 0%

profile of v1, /device:TPU:0, one launch (start us, length us, event | category | flops | bytes accessed | tf_op | source)
XLA Modules:
  0.0 352.7 jit_solution(8685204180886014605)
XLA Ops:
  0.0 1.7 bitcast_dynamic-update-slice_fusion.15
  1.7 1.7 bitcast_dynamic-update-slice_fusion.14
  20.0 1.7 bitcast_dynamic-update-slice_fusion.3
  26.7 7.3 %all-to-all-start = ((bf16[16,4,16,2048]{3,2,1,0:T(8,128)(2,1)}), bf16[16,4,16,2048]{3,2,1,0:T(8,128)(2,1)}, u32[]{:S(2)}, u32[]{:S(2)}) async-start(bf16[16,4,16,2048]{3,2,1,0:T(8,128)(2,1)} %bitcast_dynamic-update-slice_fusion), calls=%async_computation | async-start | bytes 8388608 | tf_op jit(solution)/shard_map/all_to_all | solution.py:29
  34.5 62.8 %all-to-all-done = bf16[16,4,16,2048]{3,2,1,0:T(8,128)(2,1)} async-done(((bf16[16,4,16,2048]{3,2,1,0:T(8,128)(2,1)}), bf16[16,4,16,2048]{3,2,1,0:T(8,128)(2,1)}, u32[]{:S(2)}, u32[]{:S(2)}) %all-to-all-start) | async-done | bytes 4194336 | tf_op jit(solution)/shard_map/all_to_all | solution.py:29
  97.3 2.9 convert_reduce_fusion.1
  100.3 3.6 %fusion.13 = f32[1024,32]{1,0:T(8,128)S(1)} fusion(bf16[1024,2048]{1,0:T(8,128)(2,1)} %bitcast.18, s32[2048]{0:T(1024)S(1)} %add_select_fusion), kind=kOutput, calls=%fused_computation.25 | convolution fusion | flops 134283264 | bytes 4333568 | tf_op jit(solution)/shard_map/dot_general | solution.py:18
  104.1 1.8 fusion.55
  106.8 65.2 %all-reduce.1 = (f32[64,64]{1,0:T(8,128)S(1)}, f32[64,64]{0,1:T(8,128)S(1)}) all-reduce(f32[64,64]{1,0:T(8,128)S(1)} %fusion.24, f32[64,64]{0,1:T(8,128)S(1)} %fusion.28), channel_id=1, replica_groups=mesh['mem'=16,'pix'=8] {'mem','pix'}, use_global_device_ids=true, to_apply=%region_4.6 | all-reduce | flops 8192 | bytes 65536 | tf_op jit(solution)/shard_map/psum | solution.py:124
  172.1 5.8 %cholesky.44 = f32[64,64]{1,0:T(8,128)S(1)} custom-call(f32[64,64]{1,0:T(8,128)S(1)} %fusion.51), custom_call_target="Cholesky" | custom-call | tf_op jit(solution)/shard_map/jit(cholesky)/cholesky | solution.py:76
  179.3 4.9 %custom-call.8 = f32[1,64,64]{1,2,0:T(8,128)S(1)} custom-call(f32[1,64,64]{2,1,0:T(8,128)S(1)} %fusion.42), custom_call_target="InvertDiagBlocksLowerTriangular" | custom-call | tf_op jit(solution)/shard_map/jit(_cho_solve)/triangular_solve | solution.py:78
  184.6 3.3 convert_element_type.86
  187.9 5.0 %copy.53 = f32[8,8,16,2048]{3,1,2,0:T(8,128)S(1)} copy(f32[8,8,16,2048]{3,2,1,0:T(8,128)S(1)} %bitcast.125) | data formatting | bytes 16777216
  192.9 2.6 subtract_convert_fusion
  195.5 8.5 %convert_reduce_fusion = (f32[16,2048]{1,0:T(8,128)S(1)}, bf16[64,16,2048]{2,0,1:T(8,128)(2,1)S(1)}) fusion(bf16[64,64,1]{1,0,2:T(8,128)(2,1)S(1)} %fusion.11, bf16[8,16,8,2048]{3,2,1,0:T(8,128)(2,1)} %bitcast.130, f32[64,16,2048]{2,1,0:T(8,128)S(1)} %bitcast.126), kind=kOutput, calls=%fused_computation.2 | convolution fusion | flops 276791296 | bytes 16916480 | tf_op jit(solution)/shard_map/dot_general | solution.py:86
  204.0 2.3 copy.31
  208.0 1.8 fusion.56
  211.7 64.1 %all-reduce = (f32[64,64]{1,0:T(8,128)S(1)}, f32[64,64]{0,1:T(8,128)S(1)}) all-reduce(f32[64,64]{1,0:T(8,128)S(1)} %fusion.19, f32[64,64]{0,1:T(8,128)S(1)} %fusion.29), channel_id=1, replica_groups=mesh['mem'=16,'pix'=8] {'mem','pix'}, use_global_device_ids=true, to_apply=%region_8.11 | all-reduce | flops 8192 | bytes 65536 | tf_op jit(solution)/shard_map/psum | solution.py:124
  275.9 5.8 %cholesky.55 = f32[64,64]{1,0:T(8,128)S(1)} custom-call(f32[64,64]{1,0:T(8,128)S(1)} %fusion.47), custom_call_target="Cholesky" | custom-call | tf_op jit(solution)/shard_map/jit(cholesky)/cholesky | solution.py:76
  283.2 4.9 %custom-call.9 = f32[1,64,64]{1,2,0:T(8,128)S(1)} custom-call(f32[1,64,64]{2,1,0:T(8,128)S(1)} %fusion.43), custom_call_target="InvertDiagBlocksLowerTriangular" | custom-call | tf_op jit(solution)/shard_map/jit(_cho_solve)/triangular_solve | solution.py:78
  288.5 5.0 %fusion.1 = bf16[64,16,2048]{2,0,1:T(8,128)(2,1)S(1)} fusion(bf16[64,16,2048]{2,0,1:T(8,128)(2,1)} %copy-done, bf16[64,64,1]{1,0,2:T(8,128)(2,1)S(1)} %fusion.10, f32[16,2048]{1,0:T(8,128)S(1)} %broadcast_multiply_fusion.1), kind=kOutput, calls=%fused_computation.4 | convolution fusion | flops 281018368 | bytes 8527872 | tf_op jit(solution)/shard_map/dot_general | solution.py:86
  293.5 2.3 copy.38
  295.9 54.6 %all_to_all.23 = bf16[64,16,2048]{2,1,0:T(8,128)(2,1)S(1)} all-to-all(bf16[64,16,2048]{2,1,0:T(8,128)(2,1)S(1)} %copy.38), channel_id=1, replica_groups=mesh['mem'=16,'pix'=8] {'mem'}, dimensions={0} | all-to-all | bytes 8388608 | tf_op jit(solution)/shard_map/all_to_all | solution.py:41
  350.4 2.3 copy.52
  (59 shorter events, 30.5 us)
Async XLA Ops:
  26.7 7.4 %copy-start.1 = (s32[2,1200]{1,0:T(2,128)S(1)}, s32[2,1200]{1,0:T(2,128)}, u32[]{:S(2)}) copy-start(s32[2,1200]{1,0:T(2,128)} %param.13) | copy-start | bytes 28804
  26.7 7.5 %copy-start.3 = (s32[1200]{0:T(1024)S(1)}, s32[1200]{0:T(1024)}, u32[]{:S(2)}) copy-start(s32[1200]{0:T(1024)} %param.14) | copy-start | bytes 14404
  26.7 70.6 %all-to-all-start = ((bf16[16,4,16,2048]{3,2,1,0:T(8,128)(2,1)}), bf16[16,4,16,2048]{3,2,1,0:T(8,128)(2,1)}, u32[]{:S(2)}, u32[]{:S(2)}) async-start(bf16[16,4,16,2048]{3,2,1,0:T(8,128)(2,1)} %bitcast_dynamic-update-slice_fusion), calls=%async_computation | async-start | bytes 8388608 | tf_op jit(solution)/shard_map/all_to_all | solution.py:29
  100.2 5.6 %copy-start.2 = (f32[1200]{0:T(1024)S(1)}, f32[1200]{0:T(1024)}, u32[]{:S(2)}) copy-start(f32[1200]{0:T(1024)} %param.11) | copy-start | bytes 14404
  100.3 6.1 %copy-start.5 = (f32[1200]{0:T(1024)S(1)}, f32[1200]{0:T(1024)}, u32[]{:S(2)}) copy-start(f32[1200]{0:T(1024)} %param.10) | copy-start | bytes 14404
  104.1 2.3 copy-start.4
  204.0 2.3 copy-start
